TPU v7x, 32 devices: a whole 2x2x4 slice. The times are simulated.
32 devices in a mesh: gx: 2 (over y), gy: 4 (over x, core), gz: 4 (over z).
Axes of the slice: x: 2, y: 2, z: 4, core: 2. Of those that a mesh axis runs over, the one named last changes fastest.
Arguments:
- halo_position: float32 [3, 16, 16, 8, 128], P(None, 'gx', 'gy', 'gz'), may hold values from 0 to 1
- halo_velocity: float32 [3, 16, 16, 8, 128], P(None, 'gx', 'gy', 'gz'), may hold values from -1 to 1
- halo_mass: float32 [16, 16, 8, 128], P('gx', 'gy', 'gz'), may hold values from 0.005 to 0.08
- cell_counts: int32 [16, 16, 8], P('gx', 'gy', 'gz'), may hold values from 1 to 128, as said below
Outputs:
- predicted: float32 [3, 16, 16, 8, 128], P(None, 'gx', 'gy', 'gz')
Inputs may be any that keep to these rules, and one draw needn't show every extreme that they name: `cell_counts`: slots of a cell from its count on hold no halo.
All inputs are finite; a program needn't handle non-finite values.
Results may differ from a plain program's by a relative error of at most 0.0001.
Values sent between devices are 32-bit elements; how exact they have to be, the bound alone decides.
A program may use at most 64 MiB of HBM per device.

v0:
```python
import jax
import jax.numpy as jnp
from jax import lax
from jax.sharding import PartitionSpec as P

soft_sq = 0.01
cut_sq = 0.64
cell_cap = 64


def extended_2(cells, sides, width):
    for axis, dim in sides:
        count = lax.axis_size(axis)
        head = lax.slice_in_dim(cells, 0, width, axis=dim)
        tail = lax.slice_in_dim(cells, cells.shape[dim] - width, cells.shape[dim], axis=dim)
        cells = jnp.concatenate(
            [
                lax.ppermute(tail, axis, [(i, (i + 1) % count) for i in range(count)]),
                cells,
                lax.ppermute(head, axis, [((i + 1) % count, i) for i in range(count)]),
            ],
            axis=dim,
        )
    return cells


def pull_block(extended, targets):
    depth_x, depth_y, depth_z, slot_count = targets.shape[1:]
    running = jnp.zeros(targets.shape, jnp.float32)
    for offset_code in range(27):
        shift_x = offset_code // 9
        shift_y = offset_code // 3 % 3
        shift_z = offset_code % 3
        sources = extended[
            :,
            shift_x : shift_x + depth_x,
            shift_y : shift_y + depth_y,
            shift_z : shift_z + depth_z,
            :,
        ]
        delta_x = (sources[0] + float(shift_x - 1))[..., :, None] - targets[0][..., None, :]
        delta_y = (sources[1] + float(shift_y - 1))[..., :, None] - targets[1][..., None, :]
        delta_z = (sources[2] + float(shift_z - 1))[..., :, None] - targets[2][..., None, :]
        dist_sq = delta_x * delta_x + delta_y * delta_y + delta_z * delta_z
        inv_dist = lax.rsqrt(dist_sq + soft_sq)
        tapering = jnp.maximum(1.0 - dist_sq / cut_sq, 0.0)
        weights = (
            sources[3][..., :, None] * (inv_dist * inv_dist * inv_dist) * (tapering * tapering)
        )
        running = running + jnp.stack(
            [
                jnp.sum(weights * delta_x, axis=-2),
                jnp.sum(weights * delta_y, axis=-2),
                jnp.sum(weights * delta_z, axis=-2),
            ],
            axis=0,
        )
    return running


def pull_field(extended):
    depth_x = extended.shape[1] - 2
    depth_y = extended.shape[2] - 2
    depth_z = extended.shape[3] - 2
    group_rows = 1
    for candidate in range(1, depth_x + 1):
        if depth_x % candidate == 0 and candidate * depth_y * depth_z <= cell_cap:
            group_rows = candidate
    targets = extended[:3, 1 : group_rows + 1, 1 : depth_y + 1, 1 : depth_z + 1]
    pieces = pull_block(extended, targets)
    return pieces


def body(halo_position, halo_velocity, halo_mass, cell_counts):
    occupied = lax.broadcasted_iota(jnp.int32, halo_mass.shape, 3) < cell_counts[..., None]
    held_mass = jnp.where(occupied, halo_mass, 0.0)
    outgoing = jnp.concatenate([halo_position, held_mass[None]], axis=0)
    mass_rim = None
    first_pull = None
    second_pull = None
    for round_index in range(2):
        widened = extended_2(outgoing, (("gx", 1),), 1)
        widened = extended_2(widened, (("gy", 2),), 1)
        widened = extended_2(widened, (("gz", 3),), 1)
        if round_index == 0:
            mass_rim = widened[3:4]
            first_pull = pull_field(widened)
            outgoing = halo_position + halo_velocity + 0.5 * first_pull
        else:
            second_pull = pull_field(jnp.concatenate([widened, mass_rim], axis=0))
    predicted = halo_position + halo_velocity + first_pull / 3.0 + second_pull / 6.0
    return jnp.where(occupied[None], predicted, 0.0)


def solution(mesh):
    return jax.shard_map(
        body,
        mesh=mesh,
        in_specs=(
            P(None, "gx", "gy", "gz", None),
            P(None, "gx", "gy", "gz", None),
            P("gx", "gy", "gz", None),
            P("gx", "gy", "gz"),
        ),
        out_specs=P(None, "gx", "gy", "gz", None),
        check_vma=False,
    )
```

profile of v0, /device:TPU:0, one launch (start us, length us, event | category | flops | bytes accessed | tf_op | source)
XLA Modules:
  0.0 324.4 jit_solution(9159901370591690055)
XLA Ops:
  2.4 3.1 collective-permute-start
  7.2 2.0 collective-permute-done.1
  10.1 1.7 collective-permute-start.3
  13.8 3.7 %collective-permute-start.5 = (f32[4,10,6,1,128]{4,3,2,1,0:T(1,128)S(1)}, f32[4,10,6,1,128]{4,3,2,1,0:T(1,128)S(1)}, u32[]{:S(2)}, u32[]{:S(2)}) collective-permute-start(f32[4,10,6,1,128]{4,3,2,1,0:T(1,128)S(1)} %get-tuple-element.417), channel_id=1, source_target_pairs={{1,0},{2,1},{3,2},{0,3},{5,4},{6,5},{7,6},{4,7},{9,8},{10,9},{11,1... | collective-permute-start | bytes 368648 | tf_op jit(solution)/shard_map/ppermute | solution.py:20
  17.9 2.8 collective-permute-done.5
  20.6 4.5 %collective-permute-done.4 = f32[4,10,6,1,128]{4,3,2,1,0:T(1,128)S(1)} collective-permute-done((f32[4,10,6,1,128]{4,3,2,1,0:T(1,128)S(1)}, f32[4,10,6,1,128]{4,3,2,1,0:T(1,128)S(1)}, u32[]{:S(2)}, u32[]{:S(2)}) %collective-permute-start.4) | collective-permute-done | bytes 122912 | tf_op jit(solution)/shard_map/ppermute | solution.py:18
  26.5 16.2 %fusion.80 = (f32[8,4,2,128]{3,2,1,0:T(2,128)S(1)}, f32[8,4,2,128]{3,2,1,0:T(2,128)S(1)}, f32[8,4,2,128]{3,2,1,0:T(2,128)S(1)}, f32[8,4,2,128]{3,2,1,0:T(2,128)S...) fusion(f32[8,4,2,128]{3,2,1,0:T(2,128)S(1)} %get-tuple-element., ...), kind=kLoop, calls=%fused_computation.458 | loop fusion | flops 72278016 | bytes 688128 | tf_op jit(solution)/shard_map/reduce_sum | solution.py:52
  42.6 20.4 %fusion.2 = (f32[8,4,2,128]{3,2,1,0:T(2,128)S(1)}, f32[8,4,2,128]{3,2,1,0:T(2,128)S(1)}, f32[8,4,2,128]{3,2,1,0:T(2,128)S(1)}, f32[8,4,2,128]{3,2,1,0:T(2,128)S(...) fusion(f32[8,4,2,128]{3,2,1,0:T(2,128)S(1)} %get-tuple-element., ...), kind=kLoop, calls=%fused_computation.380 | loop fusion | flops 96370688 | bytes 1015808 | tf_op jit(solution)/shard_map/reduce_sum | solution.py:52
  63.0 20.4 %fusion.41 = (f32[8,4,2,128]{3,2,1,0:T(2,128)S(1)}, f32[8,4,2,128]{3,2,1,0:T(2,128)S(1)}, f32[8,4,2,128]{3,2,1,0:T(2,128)S(1)}, f32[8,4,2,128]{3,2,1,0:T(2,128)S...) fusion(f32[8,4,2,128]{3,2,1,0:T(2,128)S(1)} %get-tuple-element., ...), kind=kLoop, calls=%fused_computation.419 | loop fusion | flops 96370688 | bytes 1015808 | tf_op jit(solution)/shard_map/reduce_sum | solution.py:52
  83.4 20.4 %fusion.28 = (f32[8,4,2,128]{3,2,1,0:T(2,128)S(1)}, f32[8,4,2,128]{3,2,1,0:T(2,128)S(1)}, f32[8,4,2,128]{3,2,1,0:T(2,128)S(1)}, f32[8,4,2,128]{3,2,1,0:T(2,128)S...) fusion(f32[8,4,2,128]{3,2,1,0:T(2,128)S(1)} %get-tuple-element., ...), kind=kLoop, calls=%fused_computation.406 | loop fusion | flops 96370688 | bytes 1015808 | tf_op jit(solution)/shard_map/reduce_sum | solution.py:52
  103.8 20.4 %fusion.15 = (f32[8,4,2,128]{3,2,1,0:T(2,128)S(1)}, f32[8,4,2,128]{3,2,1,0:T(2,128)S(1)}, f32[8,4,2,128]{3,2,1,0:T(2,128)S(1)}, f32[8,4,2,128]{3,2,1,0:T(2,128)S...) fusion(f32[8,4,2,128]{3,2,1,0:T(2,128)S(1)} %get-tuple-element., ...), kind=kLoop, calls=%fused_computation.393 | loop fusion | flops 96370688 | bytes 1015808 | tf_op jit(solution)/shard_map/reduce_sum | solution.py:52
  124.2 20.4 %fusion.54 = (f32[8,4,2,128]{3,2,1,0:T(2,128)S(1)}, f32[8,4,2,128]{3,2,1,0:T(2,128)S(1)}, f32[8,4,2,128]{3,2,1,0:T(2,128)S(1)}, f32[8,4,2,128]{3,2,1,0:T(2,128)S...) fusion(f32[8,4,2,128]{3,2,1,0:T(2,128)S(1)} %get-tuple-element., ...), kind=kLoop, calls=%fused_computation.432 | loop fusion | flops 96370688 | bytes 1015808 | tf_op jit(solution)/shard_map/reduce_sum | solution.py:52
  144.6 20.4 %fusion.67 = (f32[8,4,2,128]{3,2,1,0:T(2,128)S(1)}, f32[8,4,2,128]{3,2,1,0:T(2,128)S(1)}, f32[8,4,2,128]{3,2,1,0:T(2,128)S(1)}, f32[8,4,2,128]{3,2,1,0:T(2,128)S...) fusion(f32[8,4,2,128]{3,2,1,0:T(2,128)S(1)} %get-tuple-element., ...), kind=kLoop, calls=%fused_computation.445 | loop fusion | flops 96370688 | bytes 1015808 | tf_op jit(solution)/shard_map/reduce_sum | solution.py:52
  170.9 1.7 collective-permute-start.9
  176.8 2.9 collective-permute-done.11
  179.7 3.4 %collective-permute-done.10 = f32[3,10,6,1,128]{4,3,2,1,0:T(1,128)S(1)} collective-permute-done((f32[3,10,6,1,128]{4,3,2,1,0:T(1,128)S(1)}, f32[3,10,6,1,128]{4,3,2,1,0:T(1,128)S(1)}, u32[]{:S(2)}, u32[]{:S(2)}) %collective-permute-start.10) | collective-permute-done | bytes 92192 | tf_op jit(solution)/shard_map/ppermute | solution.py:18
  184.0 16.0 %fusion.431 = (f32[8,4,2,128]{3,2,1,0:T(2,128)S(1)}, f32[8,4,2,128]{3,2,1,0:T(2,128)S(1)}, f32[8,4,2,128]{3,2,1,0:T(2,128)S(1)}, f32[8,4,2,128]{3,2,1,0:T(2,128)...) fusion(f32[8,4,2,128]{3,2,1,0:T(2,128)S(1)} %get-tuple-element., ...), kind=kLoop, calls=%fused_computation.809 | loop fusion | flops 72278016 | bytes 688128 | tf_op jit(solution)/shard_map/reduce_sum | solution.py:52
  200.1 20.4 %fusion.392 = (f32[8,4,2,128]{3,2,1,0:T(2,128)S(1)}, f32[8,4,2,128]{3,2,1,0:T(2,128)S(1)}, f32[8,4,2,128]{3,2,1,0:T(2,128)S(1)}, f32[8,4,2,128]{3,2,1,0:T(2,128)...) fusion(f32[8,4,2,128]{3,2,1,0:T(2,128)S(1)} %get-tuple-element., ...), kind=kLoop, calls=%fused_computation.770 | loop fusion | flops 96370688 | bytes 1015808 | tf_op jit(solution)/shard_map/reduce_sum | solution.py:52
  220.5 20.4 %fusion.379 = (f32[8,4,2,128]{3,2,1,0:T(2,128)S(1)}, f32[8,4,2,128]{3,2,1,0:T(2,128)S(1)}, f32[8,4,2,128]{3,2,1,0:T(2,128)S(1)}, f32[8,4,2,128]{3,2,1,0:T(2,128)...) fusion(f32[8,4,2,128]{3,2,1,0:T(2,128)S(1)} %get-tuple-element., ...), kind=kLoop, calls=%fused_computation.757 | loop fusion | flops 96370688 | bytes 1015808 | tf_op jit(solution)/shard_map/reduce_sum | solution.py:52
  240.8 20.4 %fusion.366 = (f32[8,4,2,128]{3,2,1,0:T(2,128)S(1)}, f32[8,4,2,128]{3,2,1,0:T(2,128)S(1)}, f32[8,4,2,128]{3,2,1,0:T(2,128)S(1)}, f32[8,4,2,128]{3,2,1,0:T(2,128)...) fusion(f32[8,4,2,128]{3,2,1,0:T(2,128)S(1)} %get-tuple-element., ...), kind=kLoop, calls=%fused_computation.744 | loop fusion | flops 96370688 | bytes 1015808 | tf_op jit(solution)/shard_map/reduce_sum | solution.py:52
  261.2 20.4 %fusion.418 = (f32[8,4,2,128]{3,2,1,0:T(2,128)S(1)}, f32[8,4,2,128]{3,2,1,0:T(2,128)S(1)}, f32[8,4,2,128]{3,2,1,0:T(2,128)S(1)}, f32[8,4,2,128]{3,2,1,0:T(2,128)...) fusion(f32[8,4,2,128]{3,2,1,0:T(2,128)S(1)} %get-tuple-element., ...), kind=kLoop, calls=%fused_computation.796 | loop fusion | flops 96370688 | bytes 1015808 | tf_op jit(solution)/shard_map/reduce_sum | solution.py:52
  281.6 20.4 %fusion.353 = (f32[8,4,2,128]{3,2,1,0:T(2,128)S(1)}, f32[8,4,2,128]{3,2,1,0:T(2,128)S(1)}, f32[8,4,2,128]{3,2,1,0:T(2,128)S(1)}, f32[8,4,2,128]{3,2,1,0:T(2,128)...) fusion(f32[8,4,2,128]{3,2,1,0:T(2,128)S(1)} %get-tuple-element., ...), kind=kLoop, calls=%fused_computation.731 | loop fusion | flops 96370688 | bytes 1015808 | tf_op jit(solution)/shard_map/reduce_sum | solution.py:52
  302.0 20.4 %fusion.405 = (f32[8,4,2,128]{3,2,1,0:T(2,128)S(1)}, f32[8,4,2,128]{3,2,1,0:T(2,128)S(1)}, f32[8,4,2,128]{3,2,1,0:T(2,128)S(1)}, f32[8,4,2,128]{3,2,1,0:T(2,128)...) fusion(f32[8,4,2,128]{3,2,1,0:T(2,128)S(1)} %get-tuple-element., ...), kind=kLoop, calls=%fused_computation.783 | loop fusion | flops 96370688 | bytes 1015808 | tf_op jit(solution)/shard_map/reduce_sum | solution.py:52
  322.4 2.0 broadcast_select_fusion
  (49 shorter events, 19.6 us)
Async XLA Ops:
  0.0 11.8 %copy-start = (f32[3,8,4,2,128]{4,3,2,1,0:T(2,128)S(1)}, f32[3,8,4,2,128]{4,3,2,1,0:T(2,128)}, u32[]{:S(2)}) copy-start(f32[3,8,4,2,128]{4,3,2,1,0:T(2,128)} %param.4) | copy-start | bytes 294916
  2.4 4.8 %collective-permute-start = (f32[4,1,4,2,128]{4,3,2,1,0:T(2,128)S(1)}, f32[4,1,4,2,128]{4,3,2,1,0:T(2,128)S(1)}, u32[]{:S(2)}, u32[]{:S(2)}) collective-permute-start(f32[4,1,4,2,128]{4,3,2,1,0:T(2,128)S(1)} %get-tuple-element.477), channel_id=1, source_target_pairs={{0,16},{16,0},{1,17},{17,1},{2,18},{18,2},{3,19},{19,3},{4,20},{20... | collective-permute-start | bytes 49160 | tf_op jit(solution)/shard_map/ppermute | solution.py:18
  5.5 3.7 %collective-permute-start.1 = (f32[4,1,4,2,128]{4,3,2,1,0:T(2,128)S(1)}, f32[4,1,4,2,128]{4,3,2,1,0:T(2,128)S(1)}, u32[]{:S(2)}, u32[]{:S(2)}) collective-permute-start(f32[4,1,4,2,128]{4,3,2,1,0:T(2,128)S(1)} %get-tuple-element.478), channel_id=1, source_target_pairs={{16,0},{0,16},{17,1},{1,17},{18,2},{2,18},{19,3},{3,19},{20,4},{4,... | collective-permute-start | bytes 49160 | tf_op jit(solution)/shard_map/ppermute | solution.py:20
  10.0 3.5 %collective-permute-start.2 = (f32[4,10,1,2,128]{4,3,2,1,0:T(2,128)S(1)}, f32[4,10,1,2,128]{4,3,2,1,0:T(2,128)S(1)}, u32[]{:S(2)}, u32[]{:S(2)}) collective-permute-start(f32[4,10,1,2,128]{4,3,2,1,0:T(2,128)S(1)} %get-tuple-element.449), channel_id=1, source_target_pairs={{0,4},{4,8},{8,12},{12,0},{1,5},{5,9},{9,13},{13,1},{2,6},{6,10},{... | collective-permute-start | bytes 122888 | tf_op jit(solution)/shard_map/ppermute | solution.py:18
  10.1 3.4 %collective-permute-start.3 = (f32[4,10,1,2,128]{4,3,2,1,0:T(2,128)S(1)}, f32[4,10,1,2,128]{4,3,2,1,0:T(2,128)S(1)}, u32[]{:S(2)}, u32[]{:S(2)}) collective-permute-start(f32[4,10,1,2,128]{4,3,2,1,0:T(2,128)S(1)} %get-tuple-element.450), channel_id=1, source_target_pairs={{4,0},{8,4},{12,8},{0,12},{5,1},{9,5},{13,9},{1,13},{6,2},{10,6},{... | collective-permute-start | bytes 122888 | tf_op jit(solution)/shard_map/ppermute | solution.py:20
  13.8 6.8 %collective-permute-start.5 = (f32[4,10,6,1,128]{4,3,2,1,0:T(1,128)S(1)}, f32[4,10,6,1,128]{4,3,2,1,0:T(1,128)S(1)}, u32[]{:S(2)}, u32[]{:S(2)}) collective-permute-start(f32[4,10,6,1,128]{4,3,2,1,0:T(1,128)S(1)} %get-tuple-element.417), channel_id=1, source_target_pairs={{1,0},{2,1},{3,2},{0,3},{5,4},{6,5},{7,6},{4,7},{9,8},{10,9},{11,1... | collective-permute-start | bytes 368648 | tf_op jit(solution)/shard_map/ppermute | solution.py:20
  17.5 7.6 %collective-permute-start.4 = (f32[4,10,6,1,128]{4,3,2,1,0:T(1,128)S(1)}, f32[4,10,6,1,128]{4,3,2,1,0:T(1,128)S(1)}, u32[]{:S(2)}, u32[]{:S(2)}) collective-permute-start(f32[4,10,6,1,128]{4,3,2,1,0:T(1,128)S(1)} %get-tuple-element.418), channel_id=1, source_target_pairs={{0,1},{1,2},{2,3},{3,0},{4,5},{5,6},{6,7},{7,4},{8,9},{9,10},{10,1... | collective-permute-start | bytes 368648 | tf_op jit(solution)/shard_map/ppermute | solution.py:18
  144.6 20.4 %copy-start.1 = (f32[3,8,4,2,128]{4,3,2,1,0:T(2,128)S(1)}, f32[3,8,4,2,128]{4,3,2,1,0:T(2,128)}, u32[]{:S(2)}) copy-start(f32[3,8,4,2,128]{4,3,2,1,0:T(2,128)} %param.5) | copy-start | bytes 294916
  166.6 3.8 %collective-permute-start.6 = (f32[3,1,4,2,128]{4,3,2,1,0:T(2,128)S(1)}, f32[3,1,4,2,128]{4,3,2,1,0:T(2,128)S(1)}, u32[]{:S(2)}, u32[]{:S(2)}) collective-permute-start(f32[3,1,4,2,128]{4,3,2,1,0:T(2,128)S(1)} %get-tuple-element.495), channel_id=1, source_target_pairs={{0,16},{16,0},{1,17},{17,1},{2,18},{18,2},{3,19},{19,3},{4,20},{20... | collective-permute-start | bytes 36872 | tf_op jit(solution)/shard_map/ppermute | solution.py:18
  167.1 3.7 %collective-permute-start.7 = (f32[3,1,4,2,128]{4,3,2,1,0:T(2,128)S(1)}, f32[3,1,4,2,128]{4,3,2,1,0:T(2,128)S(1)}, u32[]{:S(2)}, u32[]{:S(2)}) collective-permute-start(f32[3,1,4,2,128]{4,3,2,1,0:T(2,128)S(1)} %get-tuple-element.496), channel_id=1, source_target_pairs={{16,0},{0,16},{17,1},{1,17},{18,2},{2,18},{19,3},{3,19},{20,4},{4,... | collective-permute-start | bytes 36872 | tf_op jit(solution)/shard_map/ppermute | solution.py:20
  170.9 3.4 %collective-permute-start.8 = (f32[3,10,1,2,128]{4,3,2,1,0:T(2,128)S(1)}, f32[3,10,1,2,128]{4,3,2,1,0:T(2,128)S(1)}, u32[]{:S(2)}, u32[]{:S(2)}) collective-permute-start(f32[3,10,1,2,128]{4,3,2,1,0:T(2,128)S(1)} %get-tuple-element.481), channel_id=1, source_target_pairs={{0,4},{4,8},{8,12},{12,0},{1,5},{5,9},{9,13},{13,1},{2,6},{6,10},{... | collective-permute-start | bytes 92168 | tf_op jit(solution)/shard_map/ppermute | solution.py:18
  170.9 3.3 %collective-permute-start.9 = (f32[3,10,1,2,128]{4,3,2,1,0:T(2,128)S(1)}, f32[3,10,1,2,128]{4,3,2,1,0:T(2,128)S(1)}, u32[]{:S(2)}, u32[]{:S(2)}) collective-permute-start(f32[3,10,1,2,128]{4,3,2,1,0:T(2,128)S(1)} %get-tuple-element.482), channel_id=1, source_target_pairs={{4,0},{8,4},{12,8},{0,12},{5,1},{9,5},{13,9},{1,13},{6,2},{10,6},{... | collective-permute-start | bytes 92168 | tf_op jit(solution)/shard_map/ppermute | solution.py:20
  174.5 5.2 %collective-permute-start.11 = (f32[3,10,6,1,128]{4,3,2,1,0:T(1,128)S(1)}, f32[3,10,6,1,128]{4,3,2,1,0:T(1,128)S(1)}, u32[]{:S(2)}, u32[]{:S(2)}) collective-permute-start(f32[3,10,6,1,128]{4,3,2,1,0:T(1,128)S(1)} %get-tuple-element.445), channel_id=1, source_target_pairs={{1,0},{2,1},{3,2},{0,3},{5,4},{6,5},{7,6},{4,7},{9,8},{10,9},{11,1... | collective-permute-start | bytes 276488 | tf_op jit(solution)/shard_map/ppermute | solution.py:20
  175.8 7.2 %collective-permute-start.10 = (f32[3,10,6,1,128]{4,3,2,1,0:T(1,128)S(1)}, f32[3,10,6,1,128]{4,3,2,1,0:T(1,128)S(1)}, u32[]{:S(2)}, u32[]{:S(2)}) collective-permute-start(f32[3,10,6,1,128]{4,3,2,1,0:T(1,128)S(1)} %get-tuple-element.446), channel_id=1, source_target_pairs={{0,1},{1,2},{2,3},{3,0},{4,5},{5,6},{6,7},{7,4},{8,9},{9,10},{10,1... | collective-permute-start | bytes 276488 | tf_op jit(solution)/shard_map/ppermute | solution.py:18
where the time goes:
time: 325 us; the launch traced here: 324 us
  other arithmetic  287 us (88%)
  waiting for transfers between devices  21.4 us (7%)
  starting transfers between devices  14.5 us (4%)
    reduce_sum x14, other arithmetic, pull_block(): jnp.sum(weights * delta_x, axis=-2)  277 us
    ppermute x6, waiting for transfers between devices, extended_2(): lax.ppermute(tail, axis, [(i, (i + 1) % count) for i in range(count)])  13.2 us
    ppermute x6, starting transfers between devices, extended_2(): lax.ppermute(head, axis, [((i + 1) % count, i) for i in range(count)])  10.1 us
    ppermute x6, waiting for transfers between devices, extended_2(): lax.ppermute(head, axis, [((i + 1) % count, i) for i in range(count)])  8.14 us
  transfers between devices with their start and end apart: 12, of which 10 were waited for; matrix products, arithmetic and copies ran while one was open for 1% of the time, Pallas kernels for 0%

commit v1 on v0

v1 whole, which is shorter than its diff:
```python
import functools
import itertools

import jax
import jax.numpy as jnp
import numpy as np
from jax import lax
from jax.experimental import pallas as pl
from jax.experimental.pallas import tpu as pltpu
from jax.sharding import PartitionSpec as P

soft_sq = 0.01
cut_sq = 0.64
scale = 1.25
soft = soft_sq * scale * scale
top = 1.0 + soft
gain = scale**3 / scale
far = 8.0
K = 48


def extended_2(cells, sides, width):
    for axis, dim in sides:
        count = lax.axis_size(axis)
        head = lax.slice_in_dim(cells, 0, width, axis=dim)
        tail = lax.slice_in_dim(cells, cells.shape[dim] - width, cells.shape[dim], axis=dim)
        cells = jnp.concatenate(
            [
                lax.ppermute(tail, axis, [(i, (i + 1) % count) for i in range(count)]),
                cells,
                lax.ppermute(head, axis, [((i + 1) % count, i) for i in range(count)]),
            ],
            axis=dim,
        )
    return cells


def parts_of(value):
    first = value.astype(jnp.bfloat16).astype(jnp.float32)
    rest = value - first
    second = rest.astype(jnp.bfloat16).astype(jnp.float32)
    third = (rest - second).astype(jnp.bfloat16).astype(jnp.float32)
    return first, second, third


def shift_tables():
    shifts = np.array(list(itertools.product((-1, 0, 1), repeat=3)), np.float32)
    offs = np.zeros((3, 32, 1), np.float32)
    offs[:, :27, 0] = scale * shifts.T
    offs = np.broadcast_to(offs, (3, 32, 128))
    rows = np.zeros((32, 16, 1), np.float32)
    for c in range(3):
        rows[:27, 3 + 3 * c : 6 + 3 * c, 0] = 2 * scale * shifts[:, c, None]
    return jnp.asarray(offs), jnp.asarray(np.broadcast_to(rows, (32, 16, 128)))


def pull_kernel(dims, src, offs, rows, out, a_scr, r_scr, t_scr, v_scr, row_scr, m_scr):
    dx, dy, dz = dims
    ey, ez = dy + 2, dz + 2
    cells = (dx + 2) * ey * ez
    ones = jnp.ones((8, 128), jnp.float32)
    zeros = jnp.zeros((8, 128), jnp.float32)
    v_scr[...] = rows[...]

    @pl.loop(0, cells // 8)
    def _(group):
        base = pl.multiple_of(group * 8, 8)
        mass = src[3, pl.ds(base, 8), :]
        a = [(src[c, pl.ds(base, 8), :] - 0.5) * scale for c in range(3)]
        a = [jnp.where(mass > 0.0, v, 0.0) for v in a]
        split = [parts_of(v) for v in a]
        norm = parts_of(a[0] * a[0] + a[1] * a[1] + a[2] * a[2])
        left = []
        for p in split:
            left += [p[0], p[0], p[1], p[0], p[2], p[1]]
        left += list(norm) + [zeros] * 11 + [ones] * 3
        for p in split:
            left += list(p)
        left += [zeros] * (K - len(left))
        for k, v in enumerate(left):
            row_scr[:, k, :] = v
        right = []
        for c in range(3):
            p = parts_of(a[c] * -2.0)
            right += [p[0], p[1], p[0], p[2], p[0], p[1]]
        right += [ones] * 3 + [zeros] * 11
        mm = [parts_of(mass * v) for v in a] + [parts_of(mass)]
        order = list(mm[0]) + list(mm[1]) + [zeros] * 2 + list(mm[2]) + list(mm[3]) + [zeros] * 2
        for k, v in enumerate(order):
            m_scr[:, k, :] = v
        for j in range(8):
            a_scr[base + j] = row_scr[j].T.astype(jnp.bfloat16)
            r = m_scr[j].astype(jnp.bfloat16)
            r_scr[base + j] = jnp.concatenate([r, r], axis=1)
        for k, v in enumerate(right):
            row_scr[:, k, :] = v
        for j in range(8):
            t_scr[base + j] = row_scr[j, :32].astype(jnp.bfloat16)

    @pl.loop(0, dx * dy * dz)
    def _(i):
        x = i // (dy * dz)
        y = i // dz % dy
        z = i % dz
        me = ((x + 1) * ey + y + 1) * ez + z + 1
        held = src[3, pl.ds(me, 1), :] > 0.0
        t = [jnp.where(held, (src[c, pl.ds(me, 1), :] - 0.5) * scale, 0.0) for c in range(3)]
        norm = soft
        for c in range(3):
            d = t[c] - offs[c]
            norm = norm + d * d
        for k, v in enumerate(parts_of(norm)):
            v_scr[:, k, :] = v
        fixed = t_scr[me]
        reach = jnp.max(jnp.maximum(jnp.maximum(jnp.abs(t[0]), jnp.abs(t[1])), jnp.abs(t[2])))

        @pl.when(reach <= far)
        def _():
            def plane(sx, carry):
                acc, lean_x, lean_y, lean_z = carry
                total = jnp.zeros((8, 128), jnp.float32)
                for sy in range(3):
                    for sz in range(3):
                        other = ((x + sx) * ey + y + sy) * ez + z + sz
                        right = jnp.concatenate(
                            [fixed, v_scr[sx * 9 + sy * 3 + sz].astype(jnp.bfloat16)], axis=0
                        )
                        v = jnp.dot(a_scr[other], right, preferred_element_type=jnp.float32)
                        r = lax.rsqrt(v)
                        g = r * jnp.maximum(top - v, 0.0)
                        w = g * g * r
                        hi = w.astype(jnp.bfloat16)
                        lo = (w - hi.astype(jnp.float32)).astype(jnp.bfloat16)
                        f = jnp.dot(
                            r_scr[other],
                            jnp.concatenate([hi, lo], axis=0),
                            preferred_element_type=jnp.float32,
                        )
                        acc = acc + f
                        m = f[8:]
                        total = total + m
                        if sy != 1:
                            lean_y = lean_y + m * float(sy - 1)
                        if sz != 1:
                            lean_z = lean_z + m * float(sz - 1)
                lean_x = lean_x + total * (sx - 1).astype(jnp.float32)
                return acc, lean_x, lean_y, lean_z

            acc, *leans = lax.fori_loop(
                0, 3, plane, (jnp.zeros((16, 128), jnp.float32), zeros, zeros, zeros)
            )

            def three(v, k):
                return v[k : k + 1] + v[k + 1 : k + 2] + v[k + 2 : k + 3]

            m = three(acc, 11)
            for c, k in enumerate((0, 3, 8)):
                out[c, pl.ds(i, 1), :] = gain * (three(acc, k) + scale * three(leans[c], 3) - t[c] * m)

        @pl.when(reach > far)
        def _():
            def one(code, carry):
                sx, sy, sz = code // 9, code // 3 % 3, code % 3
                other = ((x + sx) * ey + y + sy) * ez + z + sz
                for k in range(4):
                    m_scr[0, k : k + 1, :] = src[k, pl.ds(other, 1), :]
                cols = m_scr[0, :8].T
                deltas = []
                q = 0.0
                for c, s in enumerate((sx, sy, sz)):
                    d = cols[:, c : c + 1] + (s - 1).astype(jnp.float32) - src[c, pl.ds(me, 1), :]
                    deltas.append(d)
                    q = q + d * d
                r = lax.rsqrt(q + soft_sq)
                taper = jnp.maximum(1.0 - q * (1.0 / cut_sq), 0.0)
                w = cols[:, 3:4] * (r * r * r) * (taper * taper)
                return tuple(
                    v + jnp.sum(w * d, axis=0, keepdims=True) for v, d in zip(carry, deltas)
                )

            zero = jnp.zeros((1, 128), jnp.float32)
            pulls = lax.fori_loop(0, 27, one, (zero, zero, zero))
            for c in range(3):
                out[c, pl.ds(i, 1), :] = pulls[c]


def pull_field(extended):
    _, ex, ey, ez, slots = extended.shape
    dims = (ex - 2, ey - 2, ez - 2)
    cells = ex * ey * ez
    offs, rows = shift_tables()
    own = dims[0] * dims[1] * dims[2]
    pulls = pl.pallas_call(
        functools.partial(pull_kernel, dims),
        out_shape=jax.ShapeDtypeStruct((3, own, slots), jnp.float32),
        in_specs=[pl.BlockSpec(memory_space=pltpu.VMEM)] * 3,
        out_specs=pl.BlockSpec(memory_space=pltpu.VMEM),
        scratch_shapes=[
            pltpu.VMEM((cells, slots, K), jnp.bfloat16),
            pltpu.VMEM((cells, 16, 2 * slots), jnp.bfloat16),
            pltpu.VMEM((cells, 32, slots), jnp.bfloat16),
            pltpu.VMEM((32, 16, slots), jnp.float32),
            pltpu.VMEM((8, K, slots), jnp.float32),
            pltpu.VMEM((8, 16, slots), jnp.float32),
        ],
        compiler_params=pltpu.CompilerParams(vmem_limit_bytes=48 * 2**20),
        name="pulls",
    )(extended.reshape(4, cells, slots), offs, rows)
    return pulls.reshape((3,) + dims + (slots,))


def body(halo_position, halo_velocity, halo_mass, cell_counts):
    occupied = lax.broadcasted_iota(jnp.int32, halo_mass.shape, 3) < cell_counts[..., None]
    held_mass = jnp.where(occupied, halo_mass, 0.0)
    outgoing = jnp.concatenate([halo_position, held_mass[None]], axis=0)
    mass_rim = None
    first_pull = None
    second_pull = None
    for round_index in range(2):
        widened = extended_2(outgoing, (("gx", 1),), 1)
        widened = extended_2(widened, (("gy", 2),), 1)
        widened = extended_2(widened, (("gz", 3),), 1)
        if round_index == 0:
            mass_rim = widened[3:4]
            first_pull = pull_field(widened)
            outgoing = halo_position + halo_velocity + 0.5 * first_pull
        else:
            second_pull = pull_field(jnp.concatenate([widened, mass_rim], axis=0))
    predicted = halo_position + halo_velocity + first_pull / 3.0 + second_pull / 6.0
    return jnp.where(occupied[None], predicted, 0.0)


def solution(mesh):
    return jax.shard_map(
        body,
        mesh=mesh,
        in_specs=(
            P(None, "gx", "gy", "gz", None),
            P(None, "gx", "gy", "gz", None),
            P("gx", "gy", "gz", None),
            P("gx", "gy", "gz"),
        ),
        out_specs=P(None, "gx", "gy", "gz", None),
        check_vma=False,
    )
```

time: 325 us -> 253 us (0.78)
  other arithmetic: 287 us -> 2.66 us
  Pallas kernels: 0 us -> 208 us
    reduce_sum x14 -> x0, other arithmetic: 277 us -> none  [pull_block(): jnp.sum(weights * delta_x, axis=-2)]
    pallas_call x0 -> x2, Pallas kernels: none -> 208 us  [pull_field(): pl.pallas_call(functools.partial(pull_kernel, dims), out_shape=jax.ShapeD...]
  transfers between devices with their start and end apart: 12 -> 12, of which waited for: 10 -> 10; matrix products, arithmetic and copies ran while one was open for 1% -> 0% of each run, Pallas kernels for 0% -> 0%
where the time goes in v1:
time: 253 us; the launch traced here: 250 us
  Pallas kernels  208 us (82%)
  waiting for transfers between devices  19.4 us (8%)
  starting transfers between devices  16.6 us (7%)
  local copies, waits for them, and re-layouts  3.22 us (1%)
  other arithmetic  2.66 us (1%)
    pallas_call x2, Pallas kernels, pull_field(): pl.pallas_call(functools.partial(pull_kernel, dims), out_shape=jax.ShapeD...  208 us
    ppermute x6, waiting for transfers between devices, extended_2(): lax.ppermute(tail, axis, [(i, (i + 1) % count) for i in range(count)])  13.5 us
    ppermute x6, starting transfers between devices, extended_2(): lax.ppermute(head, axis, [((i + 1) % count, i) for i in range(count)])  10.3 us
    ppermute x6, starting transfers between devices, extended_2(): lax.ppermute(tail, axis, [(i, (i + 1) % count) for i in range(count)])  6.26 us
    ppermute x6, waiting for transfers between devices, extended_2(): lax.ppermute(head, axis, [((i + 1) % count, i) for i in range(count)])  5.89 us
  transfers between devices with their start and end apart: 12, of which 10 were waited for; matrix products, arithmetic and copies ran while one was open for 0% of the time, Pallas kernels for 0%

profile of v1, /device:TPU:0, one launch (start us, length us, event | category | flops | bytes accessed | tf_op | source)
XLA Modules:
  0.0 250.0 jit_solution(689467359186062396)
XLA Ops:
  0.0 0.8 copy.9
  0.8 0.9 select_bitcast_fusion
  1.7 3.1 %collective-permute-start = (f32[4,1,4,2,128]{4,3,2,1,0:T(2,128)S(1)}, f32[4,1,4,2,128]{4,3,2,1,0:T(2,128)S(1)}, u32[]{:S(2)}, u32[]{:S(2)}) collective-permute-start(f32[4,1,4,2,128]{4,3,2,1,0:T(2,128)S(1)} %get-tuple-element.11), channel_id=1, source_target_pairs={{0,16},{16,0},{1,17},{17,1},{2,18},{18,2},{3,19},{19,3},{4,20},{20... | collective-permute-start | bytes 49160 | tf_op jit(solution)/shard_map/ppermute | solution.py:29
  4.9 1.6 collective-permute-done
  6.5 2.0 collective-permute-done.1
  8.6 1.7 collective-permute-start.3
  10.4 1.7 collective-permute-done.2
  12.4 1.6 collective-permute-start.4
  14.0 2.2 collective-permute-start.5
  16.2 3.6 %collective-permute-done.4 = f32[4,10,6,1,128]{4,3,2,1,0:T(1,128)S(1)} collective-permute-done((f32[4,10,6,1,128]{4,3,2,1,0:T(1,128)S(1)}, f32[4,10,6,1,128]{4,3,2,1,0:T(1,128)S(1)}, u32[]{:S(2)}, u32[]{:S(2)}) %collective-permute-start.4) | collective-permute-done | bytes 122912 | tf_op jit(solution)/shard_map/ppermute | solution.py:29
  19.8 2.7 %collective-permute-done.5 = f32[4,10,6,1,128]{4,3,2,1,0:T(1,128)S(1)} collective-permute-done((f32[4,10,6,1,128]{4,3,2,1,0:T(1,128)S(1)}, f32[4,10,6,1,128]{4,3,2,1,0:T(1,128)S(1)}, u32[]{:S(2)}, u32[]{:S(2)}) %collective-permute-start.5) | collective-permute-done | bytes 122912 | tf_op jit(solution)/shard_map/ppermute | solution.py:31
  24.0 104.0 %pulls.2 = f32[3,64,128]{2,1,0:T(8,128)S(1)} custom-call(f32[4,240,128]{2,1,0:T(8,128)S(1)} %bitcast.11, f32[3,32,128]{2,1,0:T(8,128)S(1)} %jit_solution_.12.offs, f32[32,16,128]{2,1,0:T(8,128)S(1)} %jit_solution_.13.rows), custom_call_target="tpu_custom_call" | custom-call | tf_op jit(solution)/shard_map/pulls/pallas_call | solution.py:193
  128.1 0.9 copy-done.1
  129.0 0.8 collective-permute-start.6
  129.8 1.3 collective-permute-start.7
  131.1 1.7 collective-permute-done.6
  132.7 0.7 collective-permute-done.7
  133.6 1.7 collective-permute-start.9
  135.3 1.6 collective-permute-done.8
  137.1 0.7 collective-permute-start.10
  137.8 3.2 %collective-permute-start.11 = (f32[3,10,6,1,128]{4,3,2,1,0:T(1,128)S(1)}, f32[3,10,6,1,128]{4,3,2,1,0:T(1,128)S(1)}, u32[]{:S(2)}, u32[]{:S(2)}) collective-permute-start(f32[3,10,6,1,128]{4,3,2,1,0:T(1,128)S(1)} %get-tuple-element.8), channel_id=1, source_target_pairs={{1,0},{2,1},{3,2},{0,3},{5,4},{6,5},{7,6},{4,7},{9,8},{10,9},{11,1... | collective-permute-start | bytes 276488 | tf_op jit(solution)/shard_map/ppermute | solution.py:31
  141.1 3.4 %collective-permute-done.10 = f32[3,10,6,1,128]{4,3,2,1,0:T(1,128)S(1)} collective-permute-done((f32[3,10,6,1,128]{4,3,2,1,0:T(1,128)S(1)}, f32[3,10,6,1,128]{4,3,2,1,0:T(1,128)S(1)}, u32[]{:S(2)}, u32[]{:S(2)}) %collective-permute-start.10) | collective-permute-done | bytes 92192 | tf_op jit(solution)/shard_map/ppermute | solution.py:29
  145.2 104.0 %pulls.3 = f32[3,64,128]{2,1,0:T(8,128)S(1)} custom-call(f32[4,240,128]{2,1,0:T(8,128)S(1)} %bitcast.12, f32[3,32,128]{2,1,0:T(8,128)S(1)} %jit_solution_.12.offs, f32[32,16,128]{2,1,0:T(8,128)S(1)} %jit_solution_.13.rows), custom_call_target="tpu_custom_call" | custom-call | tf_op jit(solution)/shard_map/pulls/pallas_call | solution.py:193
  249.3 0.8 add_select_fusion
  (30 shorter events, 3.2 us)
Async XLA Ops:
  0.0 1.7 copy-start
  1.7 4.8 %collective-permute-start = (f32[4,1,4,2,128]{4,3,2,1,0:T(2,128)S(1)}, f32[4,1,4,2,128]{4,3,2,1,0:T(2,128)S(1)}, u32[]{:S(2)}, u32[]{:S(2)}) collective-permute-start(f32[4,1,4,2,128]{4,3,2,1,0:T(2,128)S(1)} %get-tuple-element.11), channel_id=1, source_target_pairs={{0,16},{16,0},{1,17},{17,1},{2,18},{18,2},{3,19},{19,3},{4,20},{20... | collective-permute-start | bytes 49160 | tf_op jit(solution)/shard_map/ppermute | solution.py:29
  4.8 3.7 %collective-permute-start.1 = (f32[4,1,4,2,128]{4,3,2,1,0:T(2,128)S(1)}, f32[4,1,4,2,128]{4,3,2,1,0:T(2,128)S(1)}, u32[]{:S(2)}, u32[]{:S(2)}) collective-permute-start(f32[4,1,4,2,128]{4,3,2,1,0:T(2,128)S(1)} %get-tuple-element.12), channel_id=1, source_target_pairs={{16,0},{0,16},{17,1},{1,17},{18,2},{2,18},{19,3},{3,19},{20,4},{4,... | collective-permute-start | bytes 49160 | tf_op jit(solution)/shard_map/ppermute | solution.py:31
  8.6 3.5 %collective-permute-start.2 = (f32[4,10,1,2,128]{4,3,2,1,0:T(2,128)S(1)}, f32[4,10,1,2,128]{4,3,2,1,0:T(2,128)S(1)}, u32[]{:S(2)}, u32[]{:S(2)}) collective-permute-start(f32[4,10,1,2,128]{4,3,2,1,0:T(2,128)S(1)} %get-tuple-element.9), channel_id=1, source_target_pairs={{0,4},{4,8},{8,12},{12,0},{1,5},{5,9},{9,13},{13,1},{2,6},{6,10},{... | collective-permute-start | bytes 122888 | tf_op jit(solution)/shard_map/ppermute | solution.py:29
  8.6 3.4 %collective-permute-start.3 = (f32[4,10,1,2,128]{4,3,2,1,0:T(2,128)S(1)}, f32[4,10,1,2,128]{4,3,2,1,0:T(2,128)S(1)}, u32[]{:S(2)}, u32[]{:S(2)}) collective-permute-start(f32[4,10,1,2,128]{4,3,2,1,0:T(2,128)S(1)} %get-tuple-element.10), channel_id=1, source_target_pairs={{4,0},{8,4},{12,8},{0,12},{5,1},{9,5},{13,9},{1,13},{6,2},{10,6},{... | collective-permute-start | bytes 122888 | tf_op jit(solution)/shard_map/ppermute | solution.py:31
  12.4 7.4 %collective-permute-start.4 = (f32[4,10,6,1,128]{4,3,2,1,0:T(1,128)S(1)}, f32[4,10,6,1,128]{4,3,2,1,0:T(1,128)S(1)}, u32[]{:S(2)}, u32[]{:S(2)}) collective-permute-start(f32[4,10,6,1,128]{4,3,2,1,0:T(1,128)S(1)} %get-tuple-element.5), channel_id=1, source_target_pairs={{0,1},{1,2},{2,3},{3,0},{4,5},{5,6},{6,7},{7,4},{8,9},{9,10},{10,1... | collective-permute-start | bytes 368648 | tf_op jit(solution)/shard_map/ppermute | solution.py:29
  14.0 8.5 %collective-permute-start.5 = (f32[4,10,6,1,128]{4,3,2,1,0:T(1,128)S(1)}, f32[4,10,6,1,128]{4,3,2,1,0:T(1,128)S(1)}, u32[]{:S(2)}, u32[]{:S(2)}) collective-permute-start(f32[4,10,6,1,128]{4,3,2,1,0:T(1,128)S(1)} %get-tuple-element.6), channel_id=1, source_target_pairs={{1,0},{2,1},{3,2},{0,3},{5,4},{6,5},{7,6},{4,7},{9,8},{10,9},{11,1... | collective-permute-start | bytes 368648 | tf_op jit(solution)/shard_map/ppermute | solution.py:31
  22.5 0.7 copy-start.3
  23.2 0.7 copy-start.2
  128.1 0.9 copy-start.1
  129.0 3.8 %collective-permute-start.6 = (f32[3,1,4,2,128]{4,3,2,1,0:T(2,128)S(1)}, f32[3,1,4,2,128]{4,3,2,1,0:T(2,128)S(1)}, u32[]{:S(2)}, u32[]{:S(2)}) collective-permute-start(f32[3,1,4,2,128]{4,3,2,1,0:T(2,128)S(1)} %get-tuple-element.17), channel_id=1, source_target_pairs={{0,16},{16,0},{1,17},{17,1},{2,18},{18,2},{3,19},{19,3},{4,20},{20... | collective-permute-start | bytes 36872 | tf_op jit(solution)/shard_map/ppermute | solution.py:29
  129.8 3.7 %collective-permute-start.7 = (f32[3,1,4,2,128]{4,3,2,1,0:T(2,128)S(1)}, f32[3,1,4,2,128]{4,3,2,1,0:T(2,128)S(1)}, u32[]{:S(2)}, u32[]{:S(2)}) collective-permute-start(f32[3,1,4,2,128]{4,3,2,1,0:T(2,128)S(1)} %get-tuple-element.18), channel_id=1, source_target_pairs={{16,0},{0,16},{17,1},{1,17},{18,2},{2,18},{19,3},{3,19},{20,4},{4,... | collective-permute-start | bytes 36872 | tf_op jit(solution)/shard_map/ppermute | solution.py:31
  133.5 3.4 %collective-permute-start.8 = (f32[3,10,1,2,128]{4,3,2,1,0:T(2,128)S(1)}, f32[3,10,1,2,128]{4,3,2,1,0:T(2,128)S(1)}, u32[]{:S(2)}, u32[]{:S(2)}) collective-permute-start(f32[3,10,1,2,128]{4,3,2,1,0:T(2,128)S(1)} %get-tuple-element.13), channel_id=1, source_target_pairs={{0,4},{4,8},{8,12},{12,0},{1,5},{5,9},{9,13},{13,1},{2,6},{6,10},{... | collective-permute-start | bytes 92168 | tf_op jit(solution)/shard_map/ppermute | solution.py:29
  133.6 3.3 %collective-permute-start.9 = (f32[3,10,1,2,128]{4,3,2,1,0:T(2,128)S(1)}, f32[3,10,1,2,128]{4,3,2,1,0:T(2,128)S(1)}, u32[]{:S(2)}, u32[]{:S(2)}) collective-permute-start(f32[3,10,1,2,128]{4,3,2,1,0:T(2,128)S(1)} %get-tuple-element.14), channel_id=1, source_target_pairs={{4,0},{8,4},{12,8},{0,12},{5,1},{9,5},{13,9},{1,13},{6,2},{10,6},{... | collective-permute-start | bytes 92168 | tf_op jit(solution)/shard_map/ppermute | solution.py:31
  137.1 7.4 %collective-permute-start.10 = (f32[3,10,6,1,128]{4,3,2,1,0:T(1,128)S(1)}, f32[3,10,6,1,128]{4,3,2,1,0:T(1,128)S(1)}, u32[]{:S(2)}, u32[]{:S(2)}) collective-permute-start(f32[3,10,6,1,128]{4,3,2,1,0:T(1,128)S(1)} %get-tuple-element.7), channel_id=1, source_target_pairs={{0,1},{1,2},{2,3},{3,0},{4,5},{5,6},{6,7},{7,4},{8,9},{9,10},{10,1... | collective-permute-start | bytes 276488 | tf_op jit(solution)/shard_map/ppermute | solution.py:29
  137.8 7.1 %collective-permute-start.11 = (f32[3,10,6,1,128]{4,3,2,1,0:T(1,128)S(1)}, f32[3,10,6,1,128]{4,3,2,1,0:T(1,128)S(1)}, u32[]{:S(2)}, u32[]{:S(2)}) collective-permute-start(f32[3,10,6,1,128]{4,3,2,1,0:T(1,128)S(1)} %get-tuple-element.8), channel_id=1, source_target_pairs={{1,0},{2,1},{3,2},{0,3},{5,4},{6,5},{7,6},{4,7},{9,8},{10,9},{11,1... | collective-permute-start | bytes 276488 | tf_op jit(solution)/shard_map/ppermute | solution.py:31
